TPU v7x, 32 devices: a whole 2x2x4 slice. The times are simulated.
32 devices in a mesh: dp: 8 (over z, x), mp: 4 (over y, core).
Axes of the slice: x: 2, y: 2, z: 4, core: 2. Of those that a mesh axis runs over, the one named last changes fastest.
Arguments:
- gradients: bfloat16 [8, 3584, 14336], P(None, 'dp', 'mp'), may hold values from -60 to 60
- column_slot: int32 [8, 16], replicated, may hold values from 0 to 31, as said below
- left_roots: bfloat16 [32, 4, 4, 896, 896], P('dp', 'mp'), may hold values from -1 to 5
- right_roots: bfloat16 [32, 4, 4, 896, 896], P('dp', 'mp'), may hold values from -1 to 5
Outputs:
- update: bfloat16 [8, 3584, 14336], P(None, 'dp', 'mp')
- clip_scale: float32 [], replicated
Inputs may be any that keep to these rules, and one draw needn't show every extreme that they name: `column_slot`: block column c belongs to group c // 4; over all matrices, the entries of one group's block columns are a permutation of 0 to 31.
All inputs are finite; a program needn't handle non-finite values.
Results may differ from a plain program's by a relative error of at most 0.0049.
Values may be sent and summed in bfloat16 or wider, within the bound.
A program may use at most 256 MiB of HBM per device.

v0:
```python
import functools
import math

import jax
import jax.numpy as jnp
from jax import lax
from jax.experimental import pallas as pl
from jax.experimental.pallas import tpu as pltpu
from jax.sharding import PartitionSpec as P

rms_limit = 0.25
epsilon = 1e-06
VMEM_LIMIT = 48 * 1024 * 1024


def pack_kernel(matrix_ref, column_ref, x_ref, o_ref, s_ref):
    @pl.when(pl.program_id(0) == 0)
    def _():
        s_ref[...] = jnp.zeros_like(s_ref)

    x = x_ref[0]
    o_ref[0] = x
    wide = x.astype(jnp.float32)
    s_ref[...] += jnp.sum((wide * wide).reshape(-1, 8, wide.shape[-1]), axis=0)


def pack(gradients, matrix_of, column_of, block):
    count = matrix_of.shape[0]
    rows = gradients.shape[1]
    spec = pltpu.PrefetchScalarGridSpec(
        num_scalar_prefetch=2,
        grid=(count,),
        in_specs=[pl.BlockSpec((1, rows, block), lambda i, m, c: (m[i], 0, c[i]))],
        out_specs=[
            pl.BlockSpec((1, rows, block), lambda i, m, c: (i, 0, 0)),
            pl.BlockSpec((8, block), lambda i, m, c: (0, 0)),
        ],
    )
    size = count * rows * block
    return pl.pallas_call(
        pack_kernel,
        grid_spec=spec,
        out_shape=[
            jax.ShapeDtypeStruct((count, rows, block), gradients.dtype),
            jax.ShapeDtypeStruct((8, block), jnp.float32),
        ],
        cost_estimate=pl.CostEstimate(
            flops=2 * size, bytes_accessed=4 * size, transcendentals=0
        ),
    )(matrix_of, column_of, gradients)


def product_kernel(clip_ref, x_ref, l_ref, r_ref, o_ref):
    block = l_ref.shape[-1]
    x = x_ref[...].reshape(block, block)
    first = jnp.dot(l_ref[0, 0, 0], x, preferred_element_type=jnp.float32)
    scaled = (clip_ref[0] * first).astype(jnp.bfloat16)
    second = jnp.dot(scaled, r_ref[0, 0, 0], preferred_element_type=jnp.float32)
    o_ref[...] = second.astype(o_ref.dtype).reshape(o_ref.shape)


def products(clip, received, left_roots, right_roots, first_slot):
    peers, slots, rows, block = received.shape
    row_blocks = left_roots.shape[2]
    per_block = block // rows
    root_spec = pl.BlockSpec(
        (1, 1, 1, block, block), lambda s, r: (first_slot + s, 0, r, 0, 0)
    )
    block_spec = pl.BlockSpec((per_block, 1, rows, block), lambda s, r: (r, s, 0, 0))
    count = slots * row_blocks
    return pl.pallas_call(
        product_kernel,
        grid=(slots, row_blocks),
        in_specs=[
            pl.BlockSpec(memory_space=pltpu.SMEM),
            block_spec,
            root_spec,
            root_spec,
        ],
        out_specs=block_spec,
        out_shape=jax.ShapeDtypeStruct(received.shape, received.dtype),
        compiler_params=pltpu.CompilerParams(vmem_limit_bytes=VMEM_LIMIT),
        cost_estimate=pl.CostEstimate(
            flops=4 * count * block**3,
            bytes_accessed=8 * count * block**2,
            transcendentals=0,
        ),
    )(clip, received, left_roots, right_roots)


def unpack_kernel(matrix_ref, column_ref, x_ref, *refs):
    refs[-1][0] = x_ref[0]


def unpack(returned, matrix_of, column_of, shape, partial):
    count, rows, block = returned.shape
    in_specs = [pl.BlockSpec((1, rows, block), lambda i, m, c: (i, 0, 0))]
    operands = [matrix_of, column_of, returned]
    aliases = {}
    if partial is not None:
        in_specs.append(pl.BlockSpec(memory_space=pl.ANY))
        operands.append(partial)
        aliases = {3: 0}
    spec = pltpu.PrefetchScalarGridSpec(
        num_scalar_prefetch=2,
        grid=(count,),
        in_specs=in_specs,
        out_specs=pl.BlockSpec((1, rows, block), lambda i, m, c: (m[i], 0, c[i])),
    )
    size = count * rows * block
    return pl.pallas_call(
        unpack_kernel,
        grid_spec=spec,
        out_shape=jax.ShapeDtypeStruct(shape, returned.dtype),
        input_output_aliases=aliases,
        cost_estimate=pl.CostEstimate(
            flops=0, bytes_accessed=4 * size, transcendentals=0
        ),
    )(*operands)


def body(peers, total, gradients, column_slot, left_roots, right_roots):
    matrices, rows, width = gradients.shape
    owned, block = left_roots.shape[0], left_roots.shape[-1]
    local_cols = width // block
    chunks = 2 if owned % 2 == 0 else 1
    per = owned // chunks
    slot_count = matrices * local_cols
    mp_index = lax.axis_index("mp")
    my_slots = lax.dynamic_slice_in_dim(
        column_slot, mp_index * local_cols, local_cols, 1
    ).reshape(slot_count)
    ids = jnp.arange(slot_count, dtype=jnp.int32)
    order = jnp.sum(jnp.where(my_slots[None, :] == ids[:, None], ids[None, :], 0), axis=1)
    order = order.astype(jnp.int32).reshape(peers, chunks, per)
    matrix_of = [(order[:, k] // local_cols).reshape(-1) for k in range(chunks)]
    column_of = [(order[:, k] % local_cols).reshape(-1) for k in range(chunks)]

    packed, sums = [], []
    for k in range(chunks):
        chunk, partial = pack(gradients, matrix_of[k], column_of[k], block)
        packed.append(chunk)
        sums.append(partial)
    square_sum = lax.psum(jnp.sum(functools.reduce(jnp.add, sums)), ("dp", "mp"))
    clip_scale = jnp.minimum(
        jnp.float32(1.0), rms_limit / jnp.sqrt(square_sum / total + epsilon)
    )
    clip_scale, *packed = lax.optimization_barrier((clip_scale, *packed))
    clip = clip_scale.reshape(1)
    exchange = functools.partial(
        lax.all_to_all, axis_name="dp", split_axis=0, concat_axis=0, tiled=True
    )
    received = [exchange(c) for c in packed]
    returned = []
    for k in range(chunks):
        grid = received[k].reshape(peers, per, rows, block)
        finished = products(clip, grid, left_roots, right_roots, k * per)
        returned.append(exchange(finished.reshape(peers * per, rows, block)))
    update = None
    for k in range(chunks):
        update = unpack(returned[k], matrix_of[k], column_of[k], gradients.shape, update)
    return (update, clip_scale)


def solution(mesh):
    def run(gradients, column_slot, left_roots, right_roots):
        mapped = jax.shard_map(
            functools.partial(body, mesh.shape["dp"], math.prod(gradients.shape)),
            mesh=mesh,
            in_specs=(
                P(None, "dp", "mp"),
                P(),
                P("dp", "mp", None, None, None),
                P("dp", "mp", None, None, None),
            ),
            out_specs=(P(None, "dp", "mp"), P()),
            check_vma=False,
        )
        return mapped(gradients, column_slot, left_roots, right_roots)

    return run
```

profile of v0, /device:TPU:8, one launch (start us, length us, event | category | flops | bytes accessed | tf_op | source)
XLA Modules:
  0.0 1227.8 jit_solution(18430660530258803969)
XLA Ops:
  0.6 0.0 copy-start
  0.7 0.7 copy-done
  1.3 0.1 constant_dynamic-slice_fusion
  1.4 0.1 eq.18
  1.5 0.1 select_reduce_fusion
  1.6 0.1 reshape.31
  1.7 0.1 squeeze.9
  1.8 0.1 squeeze.8
  1.9 0.5 and_select_fusion.2
  2.4 0.5 and_select_fusion
  3.0 16.0 %shard_map.59 = (bf16[16,448,896]{2,1,0:T(8,128)(2,1)}, f32[8,896]{1,0:T(8,128)}) custom-call(s32[16]{0:T(128)} %get-tuple-element.19.matrix_ref, s32[16]{0:T(128)} %get-tuple-element.18.column_ref, bf16[8,448,3584]{2,1,0:T(8,128)(2,1)} %x_ref.3), custom_call_target="tpu_custom_call" | custom-call | flops 12845056 | bytes 25690112 | tf_op jit(solution)/shard_map/pallas_call | solution.py:40
  18.9 0.0 copy-start.2
  18.9 16.2 %shard_map.60 = (bf16[16,448,896]{2,1,0:T(8,128)(2,1)}, f32[8,896]{1,0:T(8,128)}) custom-call(s32[16]{0:T(128)} %get-tuple-element.21.matrix_ref, s32[16]{0:T(128)} %get-tuple-element.20.column_ref, bf16[8,448,3584]{2,1,0:T(8,128)(2,1)} %x_ref.3), custom_call_target="tpu_custom_call" | custom-call | flops 12845056 | bytes 25690112 | tf_op jit(solution)/shard_map/pallas_call | solution.py:40
  35.1 0.0 copy-done.2
  35.1 1.4 add_reduce_fusion
  36.5 40.6 %psum.7 = f32[]{:T(128)} all-reduce(f32[]{:T(128)} %add_reduce_fusion), channel_id=1, replica_groups=mesh['dp'=8,'mp'=4] {'dp','mp'}, use_global_device_ids=true, to_apply=%region_2.3 | all-reduce | flops 1 | bytes 8 | tf_op jit(solution)/shard_map/psum | solution.py:144
  77.8 284.6 %all_to_all.20 = bf16[16,448,896]{2,1,0:T(8,128)(2,1)} all-to-all(bf16[16,448,896]{2,1,0:T(8,128)(2,1)} %get-tuple-element.15), channel_id=1, replica_groups=mesh['dp'=8,'mp'=4] {'dp'}, dimensions={0} | all-to-all | bytes 25690112 | tf_op jit(solution)/shard_map/all_to_all | solution.py:153
  362.4 6.7 all-to-all-start
  369.1 34.6 %shard_map.62 = bf16[8,2,448,896]{3,2,1,0:T(8,128)(2,1)} custom-call(f32[1]{0:T(128)} %bitcast.clip_ref, bf16[8,2,448,896]{3,2,1,0:T(8,128)(2,1)} %bitcast.7, bf16[4,1,4,896,896]{4,3,2,1,0:T(8,128)(2,1)} %l_ref.3, bf16[4,1,4,896,896]{4,3,2,1,0:T(8,128)(2,1)} %r_ref.3), custom_call_target="tpu_custom_call" | custom-call | flops 23018340352 | bytes 51380224 | tf_op jit(solution)/shard_map/pallas_call | solution.py:71
  403.7 240.6 %all-to-all-done = bf16[16,448,896]{2,1,0:T(8,128)(2,1)} async-done(((bf16[16,448,896]{2,1,0:T(8,128)(2,1)}), bf16[16,448,896]{2,1,0:T(8,128)(2,1)}, u32[]{:S(2)}, u32[]{:S(2)}) %all-to-all-start) | async-done | bytes 12845088 | tf_op jit(solution)/shard_map/all_to_all | solution.py:153
  644.3 7.8 all-to-all-start.3
  652.2 34.7 %shard_map.61 = bf16[8,2,448,896]{3,2,1,0:T(8,128)(2,1)} custom-call(f32[1]{0:T(128)} %bitcast.clip_ref, bf16[8,2,448,896]{3,2,1,0:T(8,128)(2,1)} %bitcast.1.x_ref, bf16[4,1,4,896,896]{4,3,2,1,0:T(8,128)(2,1)} %l_ref.3, bf16[4,1,4,896,896]{4,3,2,1,0:T(8,128)(2,1)} %r_ref.3), custom_call_target="tpu_custom_call" | custom-call | flops 23018340352 | bytes 51380224 | tf_op jit(solution)/shard_map/pallas_call | solution.py:71
  686.9 240.6 %all-to-all-done.3.x_ref = bf16[16,448,896]{2,1,0:T(8,128)(2,1)} async-done(((bf16[16,448,896]{2,1,0:T(8,128)(2,1)}), bf16[16,448,896]{2,1,0:T(8,128)(2,1)}, u32[]{:S(2)}, u32[]{:S(2)}) %all-to-all-start.3) | async-done | bytes 12845088 | tf_op jit(solution)/shard_map/all_to_all | solution.py:158
  927.5 7.1 all-to-all-start.1
  934.6 16.0 %shard_map.63.refs_0_ = bf16[8,448,3584]{2,1,0:T(8,128)(2,1)} custom-call(s32[16]{0:T(128)} %get-tuple-element.19.matrix_ref, s32[16]{0:T(128)} %get-tuple-element.18.column_ref, bf16[16,448,896]{2,1,0:T(8,128)(2,1)} %all-to-all-done.3.x_ref), custom_call_target="tpu_custom_call" | custom-call | bytes 25690112 | tf_op jit(solution)/shard_map/pallas_call | solution.py:111
  950.6 260.0 %all-to-all-done.1.x_ref = bf16[16,448,896]{2,1,0:T(8,128)(2,1)} async-done(((bf16[16,448,896]{2,1,0:T(8,128)(2,1)}), bf16[16,448,896]{2,1,0:T(8,128)(2,1)}, u32[]{:S(2)}, u32[]{:S(2)}) %all-to-all-start.1) | async-done | bytes 12845088 | tf_op jit(solution)/shard_map/all_to_all | solution.py:158
  1210.6 0.0 copy-start.1
  1210.6 16.1 %shard_map.64 = bf16[8,448,3584]{2,1,0:T(8,128)(2,1)} custom-call(s32[16]{0:T(128)} %get-tuple-element.21.matrix_ref, s32[16]{0:T(128)} %get-tuple-element.20.column_ref, bf16[16,448,896]{2,1,0:T(8,128)(2,1)} %all-to-all-done.1.x_ref, bf16[8,448,3584]{2,1,0:T(8,128)(2,1)} %shard_map.63.refs_0_), custom_call_target="tpu_custom_call", output_to_operand_aliasing={{}: (3, {})} | custom-call | bytes 25690112 | tf_op jit(solution)/shard_map/pallas_call | solution.py:111
  1226.7 0.0 copy-done.1
  (1 shorter events, 0.0 us)
Async XLA Ops:
  0.6 0.7 copy-start
  18.9 16.2 %copy-start.2 = (f32[8,896]{1,0:T(8,128)S(1)}, f32[8,896]{1,0:T(8,128)}, u32[]{:S(2)}) copy-start(f32[8,896]{1,0:T(8,128)} %get-tuple-element.9) | copy-start | bytes 86020
  362.4 282.0 %all-to-all-start = ((bf16[16,448,896]{2,1,0:T(8,128)(2,1)}), bf16[16,448,896]{2,1,0:T(8,128)(2,1)}, u32[]{:S(2)}, u32[]{:S(2)}) async-start(bf16[16,448,896]{2,1,0:T(8,128)(2,1)} %get-tuple-element.14), calls=%async_computation | async-start | bytes 25690112 | tf_op jit(solution)/shard_map/all_to_all | solution.py:153
  644.3 283.1 %all-to-all-start.3 = ((bf16[16,448,896]{2,1,0:T(8,128)(2,1)}), bf16[16,448,896]{2,1,0:T(8,128)(2,1)}, u32[]{:S(2)}, u32[]{:S(2)}) async-start(bf16[16,448,896]{2,1,0:T(8,128)(2,1)} %bitcast.6), calls=%async_computation.3 | async-start | bytes 25690112 | tf_op jit(solution)/shard_map/all_to_all | solution.py:158
  927.5 283.1 %all-to-all-start.1 = ((bf16[16,448,896]{2,1,0:T(8,128)(2,1)}), bf16[16,448,896]{2,1,0:T(8,128)(2,1)}, u32[]{:S(2)}, u32[]{:S(2)}) async-start(bf16[16,448,896]{2,1,0:T(8,128)(2,1)} %bitcast.5), calls=%async_computation.1 | async-start | bytes 25690112 | tf_op jit(solution)/shard_map/all_to_all | solution.py:158
  1210.6 16.1 %copy-start.1 = (s32[8,16]{1,0:T(8,128)S(1)}, s32[8,16]{1,0:T(8,128)}, u32[]{:S(2)}) copy-start(s32[8,16]{1,0:T(8,128)} %param.5) | copy-start | bytes 1540
where the time goes:
time: 1230 us
  waiting for transfers between devices  741 us (60%)
  blocking collectives  325 us (26%)
  Pallas kernels  134 us (11%)
  starting transfers between devices  21.7 us (2%)
    all_to_all x2, waiting for transfers between devices, body(): returned.append(exchange(finished.reshape(peers * per, rows, block)))  501 us
    all_to_all x1, blocking collectives, body(): received = [exchange(c) for c in packed]  285 us
    all_to_all x1, waiting for transfers between devices, body(): received = [exchange(c) for c in packed]  241 us
    pallas_call x2, Pallas kernels, products(): pl.pallas_call(product_kernel, grid=(slots, row_blocks), in_specs=[pl.Blo...  69.3 us
    psum x1, blocking collectives, body(): lax.psum(jnp.sum(functools.reduce(jnp.add, sums)), ('dp', 'mp'))  40.6 us
    pallas_call x2, Pallas kernels, pack(): pl.pallas_call(pack_kernel, grid_spec=spec, out_shape=[jax.ShapeDtypeStru...  32.1 us
    pallas_call x2, Pallas kernels, unpack(): pl.pallas_call(unpack_kernel, grid_spec=spec, out_shape=jax.ShapeDtypeStr...  32.1 us
  transfers between devices with their start and end apart: 3, of which 3 were waited for; matrix products, arithmetic and copies ran while one was open for 0% of the time, Pallas kernels for 7%

commit v1 on v0

v1 whole, which is shorter than its diff:
```python
import functools
import math

import jax
import jax.numpy as jnp
from jax import lax
from jax.experimental import pallas as pl
from jax.experimental.pallas import tpu as pltpu
from jax.sharding import PartitionSpec as P

rms_limit = 0.25
epsilon = 1e-06
MESH = pl.DeviceIdType.MESH
MIB = 1024 * 1024
LANES = 128
RING = 8


def partner(a, b, n):
    if n & (n - 1):
        return (a + b) % n
    total, bit = 0, 1
    while bit < n:
        total = total + ((a // bit + b // bit) % 2) * bit
        bit *= 2
    return total


def first_kernel(owned, slot_ref, g_ref, packed_ref, table_ref, buf, in_sem, out_sem):
    matrices, rows, width = g_ref.shape
    block = packed_ref.shape[-1]
    peers = packed_ref.shape[0]
    cols = width // block
    base = lax.axis_index("mp") * cols
    for m in range(matrices):
        for c in range(cols):
            s = slot_ref[m, base + c]
            table_ref[s] = m * cols + c

    def read(q):
        m, c = table_ref[q * owned] // cols, table_ref[q * owned] % cols
        src = g_ref.at[m, :, pl.ds(pl.multiple_of(c * block, LANES), block)]
        return pltpu.make_async_copy(src, buf.at[q], in_sem.at[q])

    def write(q):
        return pltpu.make_async_copy(buf.at[q], packed_ref.at[q, 0], out_sem.at[q])

    for q in range(peers):
        read(q).start()
    for q in range(peers):
        read(q).wait()
        write(q).start()
    for q in range(peers):
        write(q).wait()


def first_pack(column_slot, gradients, peers, owned, block):
    rows = gradients.shape[1]
    half = peers * rows * block
    return pl.pallas_call(
        functools.partial(first_kernel, owned),
        in_specs=[
            pl.BlockSpec(memory_space=pltpu.SMEM),
            pl.BlockSpec(memory_space=pltpu.HBM),
        ],
        out_specs=[
            pl.BlockSpec(memory_space=pltpu.HBM),
            pl.BlockSpec(memory_space=pltpu.SMEM),
        ],
        out_shape=[
            pltpu.HBM((peers, owned, rows, block), gradients.dtype),
            pltpu.SMEM((peers * owned,), jnp.int32),
        ],
        scratch_shapes=[
            pltpu.VMEM((peers, rows, block), gradients.dtype),
            pltpu.SemaphoreType.DMA((peers,)),
            pltpu.SemaphoreType.DMA((peers,)),
        ],
        compiler_params=pltpu.CompilerParams(vmem_limit_bytes=56 * MIB),
        cost_estimate=pl.CostEstimate(flops=0, bytes_accessed=4 * half, transcendentals=0),
    )(column_slot, gradients)


def main_kernel(
    total,
    n_mp,
    table_ref,
    packed_in,
    g_ref,
    left_ref,
    right_ref,
    packed,
    returned,
    clip_out,
    received,
    results,
    ga,
    gb,
    stage,
    acc,
    part,
    sums_dp,
    sums_mp,
    x_buf,
    l_buf,
    r_buf,
    o_buf,
    g_sem,
    stage_sem,
    block_sem,
    send_f,
    recv_f,
    send_r,
    recv_r,
    send_dp,
    recv_dp,
    send_mp,
    recv_mp,
):
    del packed_in
    peers, owned, rows, block = packed.shape
    matrices, _, width = g_ref.shape
    row_blocks = left_ref.shape[2]
    halves = block // rows
    me, mp = lax.axis_index("dp"), lax.axis_index("mp")
    my_block, my_half = me // halves, me % halves

    def peer(zo, ho):
        return partner(my_block, zo, row_blocks) * halves + partner(my_half, ho, halves)

    barrier = pltpu.get_barrier_semaphore()
    for o in range(1, peers):
        q = (me + o) % peers
        pl.semaphore_signal(barrier, inc=1, device_id=(q, mp), device_id_type=MESH)
    for o in range(1, n_mp):
        q = (mp + o) % n_mp
        pl.semaphore_signal(barrier, inc=1, device_id=(me, q), device_id_type=MESH)
    pl.semaphore_wait(barrier, peers + n_mp - 2)

    def forward(q, j):
        return pltpu.make_async_remote_copy(
            src_ref=packed.at[q, j],
            dst_ref=received.at[me, j],
            send_sem=send_f.at[q, j],
            recv_sem=recv_f.at[me, j],
            device_id=(q, mp),
            device_id_type=MESH,
        )

    def arrival(q, j):
        return pltpu.make_async_remote_copy(
            src_ref=packed.at[q, j],
            dst_ref=received.at[q, j],
            send_sem=send_f.at[q, j],
            recv_sem=recv_f.at[q, j],
            device_id=(q, mp),
            device_id_type=MESH,
        )

    order = [(zo, ho) for zo in range(1, row_blocks) for ho in range(halves)]
    order = order[len(order) // 3 :] + order[: len(order) // 3]
    order = order + [(0, ho) for ho in range(1, halves)]
    for zo, ho in order:
        forward(peer(zo, ho), 0).start()

    chunk = ga.shape[1]
    cols = width // block
    chunks = rows // chunk
    rest = peers * (owned - 1)
    acc[...] = jnp.zeros_like(acc)

    def load(t):
        buf = ga if t % 2 == 0 else gb

        def column(i, _):
            at = pl.multiple_of((i % cols) * block, LANES)
            src = g_ref.at[i // cols, pl.ds(t * chunk, chunk), pl.ds(at, block)]
            pltpu.make_async_copy(src, buf.at[i], g_sem.at[t % 2]).start()
            return 0

        lax.fori_loop(0, matrices * cols, column, 0)

    def loaded(t):
        buf = ga if t % 2 == 0 else gb
        pltpu.make_async_copy(buf, buf, g_sem.at[t % 2]).wait()

    load(0)
    for t in range(chunks):
        g = ga if t % 2 == 0 else gb
        if t + 1 < chunks:
            load(t + 1)
        loaded(t)

        def stored(n, t=t):
            q, j = n // (owned - 1), 1 + n % (owned - 1)
            return pltpu.make_async_copy(
                stage.at[n % RING],
                packed.at[q, j, pl.ds(t * chunk, chunk), :],
                stage_sem.at[n % RING],
            )

        def move(n, _, g=g, stored=stored):
            q, j = n // (owned - 1), 1 + n % (owned - 1)

            @pl.when(n >= RING)
            def _():
                stored(n - RING).wait()

            stage[n % RING] = g[table_ref[q * owned + j]]
            stored(n).start()
            return 0

        def square(n, _, g=g):
            per = chunk // 16
            x = g[n // per, pl.ds(pl.multiple_of((n % per) * 16, 16), 16), :]
            wide = x.astype(jnp.float32)
            wide = wide * wide
            acc[...] += wide[:8] + wide[8:]
            return 0

        if rest:
            lax.fori_loop(0, rest, move, 0)
        lax.fori_loop(0, matrices * cols * (chunk // 16), square, 0)
        for n in range(max(rest - RING, 0), rest):
            stored(n).wait()

    for j in range(1, owned):
        for zo, ho in order:
            forward(peer(zo, ho), j).start()

    tile = acc[:, :LANES]
    for k in range(1, block // LANES):
        tile += acc[:, k * LANES : (k + 1) * LANES]
    part[0] = tile
    sums_dp[me] = tile

    def spread(o, axis_me, n, src, dst, send, recv, device):
        q = (axis_me + o) % n
        return pltpu.make_async_remote_copy(
            src_ref=src,
            dst_ref=dst.at[axis_me],
            send_sem=send.at[o],
            recv_sem=recv.at[axis_me],
            device_id=device(q),
            device_id_type=MESH,
        )

    def landed(o, axis_me, n, src, dst, send, recv, device):
        q = (axis_me + o) % n
        return pltpu.make_async_remote_copy(
            src_ref=src,
            dst_ref=dst.at[q],
            send_sem=send.at[o],
            recv_sem=recv.at[q],
            device_id=device(q),
            device_id_type=MESH,
        )

    dp_args = (me, peers, part.at[0], sums_dp, send_dp, recv_dp, lambda q: (q, mp))
    mp_args = (mp, n_mp, part.at[1], sums_mp, send_mp, recv_mp, lambda q: (me, q))
    for o in range(1, peers):
        spread(o, *dp_args).start()
    for o in range(1, peers):
        landed(o, *dp_args).wait_recv()
    tile = jnp.sum(sums_dp[...], axis=0)
    part[1] = tile
    sums_mp[mp] = tile
    for o in range(1, n_mp):
        spread(o, *mp_args).start()
    for o in range(1, n_mp):
        landed(o, *mp_args).wait_recv()
    tile = jnp.sum(sums_mp[...], axis=0)
    square_sum = jnp.sum(jnp.sum(tile, axis=0, keepdims=True), axis=1, keepdims=True)
    clip = jnp.minimum(1.0, rms_limit / jnp.sqrt(square_sum / total + epsilon))
    clip_out[...] = jnp.broadcast_to(clip, clip_out.shape)
    for o in range(1, peers):
        spread(o, *dp_args).wait_send()
    for o in range(1, n_mp):
        spread(o, *mp_args).wait_send()

    def ret(q, j, r, h):
        return pltpu.make_async_remote_copy(
            src_ref=results.at[j, r, pl.ds(h * rows, rows), :],
            dst_ref=returned.at[me, j],
            send_sem=send_r.at[q, j],
            recv_sem=recv_r.at[me, j],
            device_id=(q, mp),
            device_id_type=MESH,
        )

    def home(q, j):
        return pltpu.make_async_remote_copy(
            src_ref=results.at[j, 0, pl.ds(0, rows), :],
            dst_ref=returned.at[q, j],
            send_sem=send_r.at[q, j],
            recv_sem=recv_r.at[q, j],
            device_id=(q, mp),
            device_id_type=MESH,
        )

    def one_block(n, _):
        j, k = n // row_blocks, n % row_blocks
        r = partner(my_block, (k + 1) % row_blocks, row_blocks)
        left = pltpu.make_async_copy(left_ref.at[j, 0, r], l_buf, block_sem.at[0])
        right = pltpu.make_async_copy(right_ref.at[j, 0, r], r_buf, block_sem.at[1])
        left.start()
        right.start()
        for h in range(halves):
            q = r * halves + h
            dst = x_buf.at[pl.ds(h * rows, rows), :]

            @pl.when(q == me)
            def _(q=q, h=h, dst=dst):
                pltpu.make_async_copy(packed.at[q, j], dst, block_sem.at[2 + h]).start()

            @pl.when(q != me)
            def _(q=q, h=h, dst=dst):
                arrival(q, j).wait_recv()
                pltpu.make_async_copy(received.at[q, j], dst, block_sem.at[2 + h]).start()

        left.wait()
        right.wait()
        for h in range(halves):
            dst = x_buf.at[pl.ds(h * rows, rows), :]
            pltpu.make_async_copy(packed.at[0, 0], dst, block_sem.at[2 + h]).wait()
        first = jnp.dot(l_buf[...], x_buf[...], preferred_element_type=jnp.float32)
        scaled = (clip_out[0:1, 0:1] * first).astype(jnp.bfloat16)
        second = jnp.dot(scaled, r_buf[...], preferred_element_type=jnp.float32)
        o_buf[...] = second.astype(o_buf.dtype)
        out = pltpu.make_async_copy(o_buf, results.at[j, r], block_sem.at[0])
        out.start()
        out.wait()
        for h in range(halves):
            q = r * halves + h

            @pl.when(q == me)
            def _(q=q, h=h):
                src = o_buf.at[pl.ds(h * rows, rows), :]
                returned[me, j] = src[...]

            @pl.when(q != me)
            def _(q=q, h=h):
                ret(q, j, r, h).start()

        return 0

    lax.fori_loop(0, owned * row_blocks, one_block, 0)

    for j in range(owned):
        for zo, ho in order:
            q = peer(zo, ho)
            forward(q, j).wait_send()
            home(q, j).wait_recv()
            home(q, j).wait_send()


def exchange(mesh, total, table, packed, gradients, left_roots, right_roots):
    peers, owned, rows, block = packed.shape
    matrices, _, width = gradients.shape
    row_blocks = left_roots.shape[2]
    n_mp = mesh.shape["mp"]
    chunk = max(c for c in range(16, 129, 16) if rows % c == 0)
    dtype = gradients.dtype
    dma = pltpu.SemaphoreType.DMA
    count = owned * row_blocks
    anywhere = pl.BlockSpec(memory_space=pltpu.HBM)
    in_vmem = pl.BlockSpec(memory_space=pltpu.VMEM)
    outs = pl.pallas_call(
        functools.partial(main_kernel, total, n_mp),
        in_specs=[pl.BlockSpec(memory_space=pltpu.SMEM)] + [anywhere] * 4,
        out_specs=[anywhere, in_vmem, in_vmem, anywhere, anywhere],
        out_shape=[
            jax.ShapeDtypeStruct(packed.shape, dtype),
            pltpu.VMEM((peers, owned, rows, block), dtype),
            jax.ShapeDtypeStruct((8, LANES), jnp.float32),
            jax.ShapeDtypeStruct(packed.shape, dtype),
            jax.ShapeDtypeStruct((owned, row_blocks, block, block), dtype),
        ],
        scratch_shapes=[
            pltpu.VMEM((peers * owned, chunk, block), dtype),
            pltpu.VMEM((peers * owned, chunk, block), dtype),
            pltpu.VMEM((RING, chunk, block), dtype),
            pltpu.VMEM((8, block), jnp.float32),
            pltpu.VMEM((2, 8, LANES), jnp.float32),
            pltpu.VMEM((peers, 8, LANES), jnp.float32),
            pltpu.VMEM((n_mp, 8, LANES), jnp.float32),
            pltpu.VMEM((block, block), dtype),
            pltpu.VMEM((block, block), dtype),
            pltpu.VMEM((block, block), dtype),
            pltpu.VMEM((block, block), dtype),
            dma((2,)),
            dma((RING,)),
            dma((2 + block // rows,)),
            dma((peers, owned)),
            dma((peers, owned)),
            dma((peers, owned)),
            dma((peers, owned)),
            dma((peers,)),
            dma((peers,)),
            dma((n_mp,)),
            dma((n_mp,)),
        ],
        input_output_aliases={1: 0},
        compiler_params=pltpu.CompilerParams(
            collective_id=0, has_side_effects=True, vmem_limit_bytes=36 * MIB
        ),
        cost_estimate=pl.CostEstimate(
            flops=4 * count * block**3,
            bytes_accessed=8 * count * block**2,
            transcendentals=0,
        ),
    )(table, packed, gradients, left_roots, right_roots)
    return outs[1], outs[2]


def last_kernel(owned, table_ref, x_ref, o_ref, sems):
    peers, _, rows, block = x_ref.shape
    cols = o_ref.shape[2] // block

    def put(s):
        m, c = table_ref[s] // cols, table_ref[s] % cols
        dst = o_ref.at[m, :, pl.ds(pl.multiple_of(c * block, LANES), block)]
        return pltpu.make_async_copy(x_ref.at[s // owned, s % owned], dst, sems.at[s])

    for s in range(peers * owned):
        put(s).start()
    for s in range(peers * owned):
        put(s).wait()


def unpack(table, returned, shape):
    peers, owned, rows, block = returned.shape
    return pl.pallas_call(
        functools.partial(last_kernel, owned),
        in_specs=[
            pl.BlockSpec(memory_space=pltpu.SMEM),
            pl.BlockSpec(memory_space=pltpu.VMEM),
        ],
        out_specs=pl.BlockSpec(memory_space=pltpu.HBM),
        out_shape=jax.ShapeDtypeStruct(shape, returned.dtype),
        scratch_shapes=[pltpu.SemaphoreType.DMA((peers * owned,))],
        compiler_params=pltpu.CompilerParams(vmem_limit_bytes=4 * MIB),
        cost_estimate=pl.CostEstimate(
            flops=0, bytes_accessed=2 * math.prod(shape), transcendentals=0
        ),
    )(table, returned)


def body(mesh, total, gradients, column_slot, left_roots, right_roots):
    owned, block = left_roots.shape[0], left_roots.shape[-1]
    peers = mesh.shape["dp"]
    packed, table = first_pack(column_slot, gradients, peers, owned, block)
    returned, clip = exchange(
        mesh, total, table, packed, gradients, left_roots, right_roots
    )
    update = unpack(table, returned, gradients.shape)
    return (update, clip[0, 0])


def solution(mesh):
    def run(gradients, column_slot, left_roots, right_roots):
        mapped = jax.shard_map(
            functools.partial(body, mesh, math.prod(gradients.shape)),
            mesh=mesh,
            in_specs=(
                P(None, "dp", "mp"),
                P(),
                P("dp", "mp", None, None, None),
                P("dp", "mp", None, None, None),
            ),
            out_specs=(P(None, "dp", "mp"), P()),
            check_vma=False,
        )
        return mapped(gradients, column_slot, left_roots, right_roots)

    return run
```

time: 1230 us -> 1200 us (0.976)
  Pallas kernels: 134 us -> 1190 us
  waiting for transfers between devices: 741 us -> 0 us
  blocking collectives: 325 us -> 0 us
  starting transfers between devices: 21.7 us -> 0 us
    pallas_call x6 -> x3, Pallas kernels: 134 us -> 1190 us  [the longest x1 1170 us: exchange(): pl.pallas_call(functools.partial(main_kernel, total, n_mp), in_specs=[pl....]
    all_to_all x3 -> x0, waiting for transfers between devices: 741 us -> none  [the longest x2 501 us: body(): returned.append(exchange(finished.reshape(peers * per, rows, block)))]
    all_to_all x1 -> x0, blocking collectives: 285 us -> none  [body(): received = [exchange(c) for c in packed]]
    psum x1 -> x0, blocking collectives: 40.6 us -> none  [body(): lax.psum(jnp.sum(functools.reduce(jnp.add, sums)), ('dp', 'mp'))]
    all_to_all x3 -> x0, starting transfers between devices: 21.7 us -> none  [the longest x2 15 us: body(): returned.append(exchange(finished.reshape(peers * per, rows, block)))]
  transfers between devices with their start and end apart: 3 -> 0, of which waited for: 3 -> 0; matrix products, arithmetic and copies ran while one was open for 0% -> 0% of each run, Pallas kernels for 7% -> 0%
where the time goes in v1:
time: 1200 us; the launch traced here: 1190 us
  Pallas kernels  1190 us (99%)
    pallas_call x1, Pallas kernels, exchange(): pl.pallas_call(functools.partial(main_kernel, total, n_mp), in_specs=[pl....  1170 us

profile of v1, /device:TPU:8, one launch (start us, length us, event | category | flops | bytes accessed | tf_op | source)
XLA Modules:
  0.0 1190.8 jit_solution(17858006718556953623)
XLA Ops:
  0.6 6.4 shard_map.59
  7.1 1173.7 %shard_map.60 = (bf16[8,4,448,896]{3,2,1,0:T(8,128)(2,1)}, bf16[8,4,448,896]{3,2,1,0:T(8,128)(2,1)S(1)}, f32[8,128]{1,0:T(8,128)}, bf16[8,4,448,896]{3,2,1,0:T(8,128)(2,1)}, bf16[4,4,896,896]{3,2,1,0:T(8,128)(2,1)}) custom-call(s32[32]{0:T(128)S(4)} %get-tuple-element.6.table_ref, ...), custom_call_target="tpu_custom_call", output_to_operand_aliasing={{0}: (1, {})} | custom-call | flops 46036680704 | bytes 102760448 | tf_op jit(solution)/shard_map/pallas_call | solution.py:368
  1180.8 1.2 slice.3
  1182.0 8.8 shard_map.61

commit v2 on v1

--- a/solution.py
+++ b/solution.py
@@ -26,10 +26,29 @@
     return total
 
 
-def first_kernel(owned, slot_ref, g_ref, packed_ref, table_ref, buf, in_sem, out_sem):
+def peer_of(zo, ho, row_blocks, halves):
+    me, mp = lax.axis_index("dp"), lax.axis_index("mp")
+    block, half = me // halves, me % halves
+    if not (isinstance(zo, int) and zo == 0):
+        ho = (ho + mp) % halves
+    return partner(block, zo, row_blocks) * halves + partner(half, ho, halves)
+
+
+NEAR = 2
+
+
+def first_kernel(
+    owned, row_blocks, slot_ref, g_ref, packed_ref, table_ref, buf, in_sem, out_sem
+):
     matrices, rows, width = g_ref.shape
     block = packed_ref.shape[-1]
     peers = packed_ref.shape[0]
+    halves = peers // row_blocks
+    first = [
+        peer_of(zo, ho, row_blocks, halves)
+        for zo in range(NEAR, row_blocks)
+        for ho in range(halves)
+    ]
     cols = width // block
     base = lax.axis_index("mp") * cols
     for m in range(matrices):
@@ -37,28 +56,29 @@
             s = slot_ref[m, base + c]
             table_ref[s] = m * cols + c
 
-    def read(q):
-        m, c = table_ref[q * owned] // cols, table_ref[q * owned] % cols
-        src = g_ref.at[m, :, pl.ds(pl.multiple_of(c * block, LANES), block)]
-        return pltpu.make_async_copy(src, buf.at[q], in_sem.at[q])
-
-    def write(q):
-        return pltpu.make_async_copy(buf.at[q], packed_ref.at[q, 0], out_sem.at[q])
-
-    for q in range(peers):
-        read(q).start()
-    for q in range(peers):
-        read(q).wait()
-        write(q).start()
-    for q in range(peers):
-        write(q).wait()
-
-
-def first_pack(column_slot, gradients, peers, owned, block):
+    def read(k):
+        s = table_ref[first[k] * owned]
+        at = pl.multiple_of((s % cols) * block, LANES)
+        src = g_ref.at[s // cols, :, pl.ds(at, block)]
+        return pltpu.make_async_copy(src, buf.at[k], in_sem.at[k])
+
+    def write(k):
+        return pltpu.make_async_copy(buf.at[k], packed_ref.at[first[k], 0], out_sem.at[k])
+
+    for k in range(len(first)):
+        read(k).start()
+    for k in range(len(first)):
+        read(k).wait()
+        write(k).start()
+    for k in range(len(first)):
+        write(k).wait()
+
+
+def first_pack(column_slot, gradients, peers, owned, row_blocks, block):
     rows = gradients.shape[1]
     half = peers * rows * block
     return pl.pallas_call(
-        functools.partial(first_kernel, owned),
+        functools.partial(first_kernel, owned, row_blocks),
         in_specs=[
             pl.BlockSpec(memory_space=pltpu.SMEM),
             pl.BlockSpec(memory_space=pltpu.HBM),
@@ -126,7 +146,7 @@
     my_block, my_half = me // halves, me % halves
 
     def peer(zo, ho):
-        return partner(my_block, zo, row_blocks) * halves + partner(my_half, ho, halves)
+        return peer_of(zo, ho, row_blocks, halves)
 
     barrier = pltpu.get_barrier_semaphore()
     for o in range(1, peers):
@@ -157,17 +177,22 @@
             device_id_type=MESH,
         )
 
-    order = [(zo, ho) for zo in range(1, row_blocks) for ho in range(halves)]
-    order = order[len(order) // 3 :] + order[: len(order) // 3]
-    order = order + [(0, ho) for ho in range(1, halves)]
-    for zo, ho in order:
+    first = [(zo, ho) for zo in range(NEAR, row_blocks) for ho in range(halves)]
+    later = [(zo, ho) for zo in range(1, NEAR) for ho in range(halves)]
+    later = later + [(0, ho) for ho in range(1, halves)]
+    for zo, ho in first:
         forward(peer(zo, ho), 0).start()
 
     chunk = ga.shape[1]
     cols = width // block
     chunks = rows // chunk
-    rest = peers * (owned - 1)
+    rest = peers * owned - len(first)
     acc[...] = jnp.zeros_like(acc)
+
+    def unit(n):
+        n = n + len(first)
+        k = n % peers
+        return peer((k // halves + NEAR) % row_blocks, k % halves), n // peers
 
     def load(t):
         buf = ga if t % 2 == 0 else gb
@@ -192,7 +217,7 @@
         loaded(t)
 
         def stored(n, t=t):
-            q, j = n // (owned - 1), 1 + n % (owned - 1)
+            q, j = unit(n)
             return pltpu.make_async_copy(
                 stage.at[n % RING],
                 packed.at[q, j, pl.ds(t * chunk, chunk), :],
@@ -200,7 +225,7 @@
             )
 
         def move(n, _, g=g, stored=stored):
-            q, j = n // (owned - 1), 1 + n % (owned - 1)
+            q, j = unit(n)
 
             @pl.when(n >= RING)
             def _():
@@ -218,14 +243,13 @@
             acc[...] += wide[:8] + wide[8:]
             return 0
 
-        if rest:
-            lax.fori_loop(0, rest, move, 0)
+        lax.fori_loop(0, rest, move, 0)
         lax.fori_loop(0, matrices * cols * (chunk // 16), square, 0)
         for n in range(max(rest - RING, 0), rest):
             stored(n).wait()
 
-    for j in range(1, owned):
-        for zo, ho in order:
+    for j in range(owned):
+        for zo, ho in (first if j else []) + later:
             forward(peer(zo, ho), j).start()
 
     tile = acc[:, :LANES]
@@ -272,7 +296,7 @@
     tile = jnp.sum(sums_mp[...], axis=0)
     square_sum = jnp.sum(jnp.sum(tile, axis=0, keepdims=True), axis=1, keepdims=True)
     clip = jnp.minimum(1.0, rms_limit / jnp.sqrt(square_sum / total + epsilon))
-    clip_out[...] = jnp.broadcast_to(clip, clip_out.shape)
+    clip_out[0, 0] = clip[0, 0]
     for o in range(1, peers):
         spread(o, *dp_args).wait_send()
     for o in range(1, n_mp):
@@ -324,19 +348,19 @@
             dst = x_buf.at[pl.ds(h * rows, rows), :]
             pltpu.make_async_copy(packed.at[0, 0], dst, block_sem.at[2 + h]).wait()
         first = jnp.dot(l_buf[...], x_buf[...], preferred_element_type=jnp.float32)
-        scaled = (clip_out[0:1, 0:1] * first).astype(jnp.bfloat16)
+        scaled = (clip_out[0, 0] * first).astype(jnp.bfloat16)
         second = jnp.dot(scaled, r_buf[...], preferred_element_type=jnp.float32)
         o_buf[...] = second.astype(o_buf.dtype)
         out = pltpu.make_async_copy(o_buf, results.at[j, r], block_sem.at[0])
         out.start()
         out.wait()
-        for h in range(halves):
+        for t in range(halves):
+            h = partner(my_half, (t + mp) % halves, halves)
             q = r * halves + h
 
             @pl.when(q == me)
             def _(q=q, h=h):
-                src = o_buf.at[pl.ds(h * rows, rows), :]
-                returned[me, j] = src[...]
+                returned[me, j] = o_buf[pl.ds(pl.multiple_of(h * rows, 16), rows), :]
 
             @pl.when(q != me)
             def _(q=q, h=h):
@@ -347,7 +371,7 @@
     lax.fori_loop(0, owned * row_blocks, one_block, 0)
 
     for j in range(owned):
-        for zo, ho in order:
+        for zo, ho in first + later:
             q = peer(zo, ho)
             forward(q, j).wait_send()
             home(q, j).wait_recv()
@@ -365,14 +389,15 @@
     count = owned * row_blocks
     anywhere = pl.BlockSpec(memory_space=pltpu.HBM)
     in_vmem = pl.BlockSpec(memory_space=pltpu.VMEM)
+    in_smem = pl.BlockSpec(memory_space=pltpu.SMEM)
     outs = pl.pallas_call(
         functools.partial(main_kernel, total, n_mp),
         in_specs=[pl.BlockSpec(memory_space=pltpu.SMEM)] + [anywhere] * 4,
-        out_specs=[anywhere, in_vmem, in_vmem, anywhere, anywhere],
+        out_specs=[anywhere, in_vmem, in_smem, anywhere, anywhere],
         out_shape=[
             jax.ShapeDtypeStruct(packed.shape, dtype),
             pltpu.VMEM((peers, owned, rows, block), dtype),
-            jax.ShapeDtypeStruct((8, LANES), jnp.float32),
+            pltpu.SMEM((1, 1), jnp.float32),
             jax.ShapeDtypeStruct(packed.shape, dtype),
             jax.ShapeDtypeStruct((owned, row_blocks, block, block), dtype),
         ],
@@ -413,7 +438,7 @@
     return outs[1], outs[2]
 
 
-def last_kernel(owned, table_ref, x_ref, o_ref, sems):
+def last_kernel(owned, table_ref, clip_ref, x_ref, o_ref, clip_out, sems):
     peers, _, rows, block = x_ref.shape
     cols = o_ref.shape[2] // block
 
@@ -424,37 +449,47 @@
 
     for s in range(peers * owned):
         put(s).start()
+    clip_out[0, 0] = clip_ref[0, 0]
     for s in range(peers * owned):
         put(s).wait()
 
 
-def unpack(table, returned, shape):
+def unpack(table, clip, returned, shape):
     peers, owned, rows, block = returned.shape
     return pl.pallas_call(
         functools.partial(last_kernel, owned),
         in_specs=[
             pl.BlockSpec(memory_space=pltpu.SMEM),
+            pl.BlockSpec(memory_space=pltpu.SMEM),
             pl.BlockSpec(memory_space=pltpu.VMEM),
         ],
-        out_specs=pl.BlockSpec(memory_space=pltpu.HBM),
-        out_shape=jax.ShapeDtypeStruct(shape, returned.dtype),
+        out_specs=[
+            pl.BlockSpec(memory_space=pltpu.HBM),
+            pl.BlockSpec(memory_space=pltpu.SMEM),
+        ],
+        out_shape=[
+            jax.ShapeDtypeStruct(shape, returned.dtype),
+            jax.ShapeDtypeStruct((1, 1), jnp.float32),
+        ],
         scratch_shapes=[pltpu.SemaphoreType.DMA((peers * owned,))],
         compiler_params=pltpu.CompilerParams(vmem_limit_bytes=4 * MIB),
         cost_estimate=pl.CostEstimate(
             flops=0, bytes_accessed=2 * math.prod(shape), transcendentals=0
         ),
-    )(table, returned)
+    )(table, clip, returned)
 
 
 def body(mesh, total, gradients, column_slot, left_roots, right_roots):
     owned, block = left_roots.shape[0], left_roots.shape[-1]
     peers = mesh.shape["dp"]
-    packed, table = first_pack(column_slot, gradients, peers, owned, block)
+    packed, table = first_pack(
+        column_slot, gradients, peers, owned, left_roots.shape[2], block
+    )
     returned, clip = exchange(
         mesh, total, table, packed, gradients, left_roots, right_roots
     )
-    update = unpack(table, returned, gradients.shape)
-    return (update, clip[0, 0])
+    update, clip = unpack(table, clip, returned, gradients.shape)
+    return (update, clip.reshape(()))
 
 
 def solution(mesh):

time: 1200 us -> 1140 us (0.950); the launches traced: 1190 us -> 1140 us
  Pallas kernels: 1190 us -> 1140 us
    pallas_call x1, Pallas kernels: 1170 us -> 1130 us  [exchange(): pl.pallas_call(functools.partial(main_kernel, total, n_mp), in_specs=[pl....]
where the time goes in v2:
time: 1140 us
  Pallas kernels  1140 us (100%)
    pallas_call x1, Pallas kernels, exchange(): pl.pallas_call(functools.partial(main_kernel, total, n_mp), in_specs=[pl....  1130 us

profile of v2, /device:TPU:8, one launch (start us, length us, event | category | flops | bytes accessed | tf_op | source)
XLA Modules:
  0.0 1143.5 jit_solution(13293391315043942929)
XLA Ops:
  0.6 3.8 shard_map.59
  4.5 1129.8 %shard_map.60 = (bf16[8,4,448,896]{3,2,1,0:T(8,128)(2,1)}, bf16[8,4,448,896]{3,2,1,0:T(8,128)(2,1)S(1)}, f32[1,1]{1,0:T(1,128)S(4)}, bf16[8,4,448,896]{3,2,1,0:T(8,128)(2,1)}, bf16[4,4,896,896]{3,2,1,0:T(8,128)(2,1)}) custom-call(s32[32]{0:T(128)S(4)} %get-tuple-element.8.table_ref, ...), custom_call_target="tpu_custom_call", output_to_operand_aliasing={{0}: (1, {})} | custom-call | flops 46036680704 | bytes 102760448 | tf_op jit(solution)/shard_map/pallas_call | solution.py:393
  1134.2 9.3 shard_map.61

commit v3 on v2

--- a/solution.py
+++ b/solution.py
@@ -187,7 +187,6 @@
     cols = width // block
     chunks = rows // chunk
     rest = peers * owned - len(first)
-    acc[...] = jnp.zeros_like(acc)
 
     def unit(n):
         n = n + len(first)
@@ -200,21 +199,23 @@
         def column(i, _):
             at = pl.multiple_of((i % cols) * block, LANES)
             src = g_ref.at[i // cols, pl.ds(t * chunk, chunk), pl.ds(at, block)]
-            pltpu.make_async_copy(src, buf.at[i], g_sem.at[t % 2]).start()
+            pltpu.make_async_copy(src, buf.at[i], load_sem).start()
             return 0
 
+        load_sem = g_sem.at[0] if buf is ga else g_sem.at[1]
         lax.fori_loop(0, matrices * cols, column, 0)
 
     def loaded(t):
         buf = ga if t % 2 == 0 else gb
         pltpu.make_async_copy(buf, buf, g_sem.at[t % 2]).wait()
-
+        return buf
+
+    acc[...] = jnp.zeros_like(acc)
     load(0)
     for t in range(chunks):
-        g = ga if t % 2 == 0 else gb
         if t + 1 < chunks:
             load(t + 1)
-        loaded(t)
+        g = loaded(t)
 
         def stored(n, t=t):
             q, j = unit(n)
@@ -236,21 +237,14 @@
             return 0
 
         def square(n, _, g=g):
-            per = chunk // 16
-            x = g[n // per, pl.ds(pl.multiple_of((n % per) * 16, 16), 16), :]
-            wide = x.astype(jnp.float32)
-            wide = wide * wide
-            acc[...] += wide[:8] + wide[8:]
+            wide = g[n].astype(jnp.float32)
+            acc[...] += jnp.sum((wide * wide).reshape(-1, 8, block), axis=0)
             return 0
 
         lax.fori_loop(0, rest, move, 0)
-        lax.fori_loop(0, matrices * cols * (chunk // 16), square, 0)
+        lax.fori_loop(0, matrices * cols, square, 0)
         for n in range(max(rest - RING, 0), rest):
             stored(n).wait()
-
-    for j in range(owned):
-        for zo, ho in (first if j else []) + later:
-            forward(peer(zo, ho), j).start()
 
     tile = acc[:, :LANES]
     for k in range(1, block // LANES):
@@ -284,6 +278,9 @@
     mp_args = (mp, n_mp, part.at[1], sums_mp, send_mp, recv_mp, lambda q: (me, q))
     for o in range(1, peers):
         spread(o, *dp_args).start()
+    for j in range(owned):
+        for zo, ho in (first if j else []) + later:
+            forward(peer(zo, ho), j).start()
     for o in range(1, peers):
         landed(o, *dp_args).wait_recv()
     tile = jnp.sum(sums_dp[...], axis=0)

time: 1140 us -> 1120 us (0.982)
  Pallas kernels: 1140 us -> 1120 us
    pallas_call x1, Pallas kernels: 1130 us -> 1110 us  [exchange(): pl.pallas_call(functools.partial(main_kernel, total, n_mp), in_specs=[pl....]
where the time goes in v3:
time: 1120 us
  Pallas kernels  1120 us (100%)
    pallas_call x1, Pallas kernels, exchange(): pl.pallas_call(functools.partial(main_kernel, total, n_mp), in_specs=[pl....  1110 us

profile of v3, /device:TPU:8, one launch (start us, length us, event | category | flops | bytes accessed | tf_op | source)
XLA Modules:
  0.0 1122.6 jit_solution(11883666200963755641)
XLA Ops:
  0.6 3.8 shard_map.59
  4.5 1108.8 %shard_map.60 = (bf16[8,4,448,896]{3,2,1,0:T(8,128)(2,1)}, bf16[8,4,448,896]{3,2,1,0:T(8,128)(2,1)S(1)}, f32[1,1]{1,0:T(1,128)S(4)}, bf16[8,4,448,896]{3,2,1,0:T(8,128)(2,1)}, bf16[4,4,896,896]{3,2,1,0:T(8,128)(2,1)}) custom-call(s32[32]{0:T(128)S(4)} %get-tuple-element.8.table_ref, ...), custom_call_target="tpu_custom_call", output_to_operand_aliasing={{0}: (1, {})} | custom-call | flops 46036680704 | bytes 102760448 | tf_op jit(solution)/shard_map/pallas_call | solution.py:390
  1113.3 9.3 shard_map.61
